TPU v7x, 32 devices: a whole 2x2x4 slice. The times are simulated.
32 devices in a mesh: gx: 8 (over y, x, core), gy: 4 (over z).
Axes of the slice: x: 2, y: 2, z: 4, core: 2. Of those that a mesh axis runs over, the one named last changes fastest.
Arguments:
- pair_in: bfloat16 [256, 256, 128], P(('gx', 'gy')), may hold values from -6 to 6
- residue_mask: int32 [256], P(('gx', 'gy')), may hold values 0 or 1
- norm_start: float32 [128], replicated, may hold values from 0.25 to 1.75
- proj_start: bfloat16 [128, 512], replicated, may hold values from -0.5 to 0.5
- gate_bias_start: float32 [128], replicated, may hold values from -4 to 4
- bias_w_start: bfloat16 [128, 4], replicated, may hold values from -1.5 to 1.5
- out_w_start: bfloat16 [128, 128], replicated, may hold values from -1 to 1
- norm_end: float32 [128], replicated, may hold values from 0.25 to 1.75
- proj_end: bfloat16 [128, 512], replicated, may hold values from -0.5 to 0.5
- gate_bias_end: float32 [128], replicated, may hold values from -4 to 4
- bias_w_end: bfloat16 [128, 4], replicated, may hold values from -1.5 to 1.5
- out_w_end: bfloat16 [128, 128], replicated, may hold values from -1 to 1
- norm_trans: float32 [128], replicated, may hold values from 0.25 to 1.75
- trans_in: bfloat16 [128, 512], replicated, may hold values from -0.5 to 0.5
- trans_bias: float32 [512], replicated, may hold values from -4 to 4
- trans_out: bfloat16 [512, 128], replicated, may hold values from -0.375 to 0.375
Outputs:
- pair_out: bfloat16 [256, 256, 128], P(('gx', 'gy'))
Inputs may be any that keep to these rules, and one draw needn't show every extreme that they name: residue_mask holds only 0 and 1.
All inputs are finite; a program needn't handle non-finite values.
Results may differ from a plain program's by a relative error of at most 0.02.
Values may be sent and summed in bfloat16 or wider, within the bound.
A program may use at most 192 MiB of HBM per device.

v0:
```python
import jax
import jax.numpy as jnp
from jax import lax
from jax.sharding import PartitionSpec as P

HEADS = 4
HEAD_DIM = 32


big_negative = 1000000000.0


def layer_norm(values, norm_gain):
    widened = values.astype(jnp.float32)
    row_mean = jnp.mean(widened, axis=-1, keepdims=True)
    row_var = jnp.mean(jnp.square(widened - row_mean), axis=-1, keepdims=True)
    return ((widened - row_mean) * lax.rsqrt(row_var + 1e-05) * norm_gain).astype(jnp.bfloat16)


def project(normed, weight):
    flat = normed.reshape(-1, normed.shape[-1])
    result = jnp.dot(flat, weight, preferred_element_type=jnp.float32)
    return result.reshape(normed.shape[:-1] + (weight.shape[1],))


def split_heads(merged):
    return merged.astype(jnp.bfloat16).reshape(merged.shape[:-1] + (HEADS, HEAD_DIM))


def attend_block(query, keys, values, pair_bias, key_bias):
    score_scale = HEAD_DIM ** (-0.5)
    scores = jnp.einsum("jhd,khd->hjk", query, keys, preferred_element_type=jnp.float32)
    scores = scores * score_scale + pair_bias + key_bias
    attn_weights = jax.nn.softmax(scores, axis=-1)
    mixed = jnp.einsum(
        "hjk,khd->jhd", attn_weights, values.astype(jnp.float32), precision=lax.Precision.HIGHEST
    )
    return mixed.reshape(query.shape[0], HEADS * HEAD_DIM)


def gated_residual(residual, mixed, gate_logit, gate_bias, out_weight):
    gated = (mixed * jax.nn.sigmoid(gate_logit + gate_bias)).astype(jnp.bfloat16)
    return (residual.astype(jnp.float32) + project(gated, out_weight)).astype(jnp.bfloat16)


def projections(normed, weight, channels):
    projected = project(normed, weight)
    query = split_heads(projected[..., :channels])
    keys = split_heads(projected[..., channels : 2 * channels])
    values = split_heads(projected[..., 2 * channels : 3 * channels])
    return (query, keys, values, projected[..., 3 * channels :])


def local(
    pair_in,
    residue_mask,
    norm_start,
    proj_start,
    gate_bias_start,
    bias_w_start,
    out_w_start,
    norm_end,
    proj_end,
    gate_bias_end,
    bias_w_end,
    out_w_end,
    norm_trans,
    trans_in,
    trans_bias,
    trans_out,
):
    row_count, total_res, channels = pair_in.shape
    full_mask = lax.all_gather(residue_mask, ("gx", "gy"), axis=0, tiled=True)
    key_bias = (full_mask.astype(jnp.float32) - 1.0) * big_negative
    normed = layer_norm(pair_in, norm_start)
    query, keys, values, gate_logit = projections(normed, proj_start, channels)
    local_bias = project(normed, bias_w_start).astype(jnp.bfloat16)

    def start_block(portion):
        span = portion.shape[0]
        pair_bias = jnp.transpose(portion, (2, 0, 1)).astype(jnp.float32)
        query_part = lax.slice_in_dim(query, 0, span, axis=1)

        def per_row(operands):
            query_row, key_row, value_row = operands
            return attend_block(query_row, key_row, value_row, pair_bias, key_bias)

        return lax.map(per_row, (query_part, keys, values))

    mixed = start_block(lax.all_gather(local_bias, ("gx", "gy"), axis=0, tiled=True))
    after_start = gated_residual(pair_in, mixed, gate_logit, gate_bias_start, out_w_start)
    column_pair = lax.all_to_all(after_start, ("gx", "gy"), split_axis=1, concat_axis=0, tiled=True)
    normed = layer_norm(column_pair, norm_end)
    query, keys, values, gate_logit = projections(normed, proj_end, channels)
    local_bias = project(normed, bias_w_end).astype(jnp.bfloat16)
    key_cols = jnp.swapaxes(keys, 0, 1)
    value_cols = jnp.swapaxes(values, 0, 1)

    def end_block(portion):
        span = portion.shape[1]
        pair_bias = jnp.transpose(portion, (2, 1, 0)).astype(jnp.float32)
        query_part = jnp.swapaxes(lax.slice_in_dim(query, 0, span, axis=0), 0, 1)

        def per_column(operands):
            query_col, key_col, value_col = operands
            return attend_block(query_col, key_col, value_col, pair_bias, key_bias)

        return jnp.swapaxes(lax.map(per_column, (query_part, key_cols, value_cols)), 0, 1)

    mixed = end_block(lax.all_gather(local_bias, ("gx", "gy"), axis=1, tiled=True))
    after_end = gated_residual(column_pair, mixed, gate_logit, gate_bias_end, out_w_end)
    row_pair = lax.all_to_all(after_end, ("gx", "gy"), split_axis=0, concat_axis=1, tiled=True)
    normed = layer_norm(row_pair, norm_trans)
    hidden = jax.nn.relu(project(normed, trans_in) + trans_bias).astype(jnp.bfloat16)
    return (row_pair.astype(jnp.float32) + project(hidden, trans_out)).astype(jnp.bfloat16)


def solution(mesh):
    placed = (
        P(("gx", "gy"), None, None),
        P(("gx", "gy")),
        P(),
        P(),
        P(),
        P(),
        P(),
        P(),
        P(),
        P(),
        P(),
        P(),
        P(),
        P(),
        P(),
        P(),
    )
    return jax.shard_map(
        local, mesh=mesh, in_specs=placed, out_specs=P(("gx", "gy"), None, None), check_vma=False
    )
```

profile of v0, /device:TPU:0, one launch (start us, length us, event | category | flops | bytes accessed | tf_op | source)
XLA Modules:
  0.0 300.2 jit_solution(6452829403129993043)
XLA Ops:
  1.3 1.7 fusion.37
  3.0 3.7 %fusion.98 = (bf16[8,256,512]{2,1,0:T(8,128)(2,1)S(1)}, f32[8,256,512]{2,1,0:T(8,128)}) fusion(bf16[128,512]{1,0:T(8,128)(2,1)S(1)} %copy-done, bf16[8,256,128]{2,1,0:T(8,128)(2,1)} %param.20, f32[128]{0:T(128)} %param.22, f32[8,256]{1,0:T(8,128)S(1)} %add_rsqrt_fusion.2, f32[8,256]{1,0:T(8,128)S(1)} %broadcast_multiply_fusion.2), kind=kOutput, calls=%fused_computation.119 | convolution fusion | flops 270794752 | bytes 6963712 | tf_op jit(solution)/shard_map/dot_general | solution.py:22
  10.2 73.9 %all_gather.9 = bf16[256,256,4]{1,2,0:T(4,128)(2,1)S(1)} all-gather(bf16[8,256,4]{1,2,0:T(4,128)(2,1)S(1)} %convolution_convert_fusion.1), channel_id=1, replica_groups=mesh['gx'=8,'gy'=4] {'gx','gy'}, dimensions={0}, use_global_device_ids=true | all-gather | bytes 540672 | tf_op jit(solution)/shard_map/all_gather | solution.py:90
  84.9 36.8 %all-reduce = s32[256]{0:T(256)S(1)} all-reduce(s32[256]{0:T(256)S(1)} %dynamic-update-slice), channel_id=1, replica_groups=mesh['gx'=8,'gy'=4] {'gx','gy'}, use_global_device_ids=true, to_apply=%add | all-reduce | flops 256 | bytes 2048
  121.8 23.9 %while.20 = (s32[]{:T(128)}, f32[8,256,128]{2,1,0:T(8,128)S(1)}, bf16[8,256,4,32]{1,3,2,0:T(8,128)(2,1)}, bf16[8,256,4,32]{1,3,2,0:T(8,128)(2,1)S(1)}, bf16[8,25...) while((s32[]{:T(128)}, f32[8,256,128]{2,1,0:T(8,128)S(1)}, ...), condition=%wide.region_5.6_spmd, body=%wide.region_2.5_spmd.sunk | while | flops 119535616 | bytes 5069401 | solution.py:88
  123.2 1.5 fusion.114
  129.2 1.5 fusion.114
  132.2 1.5 fusion.114
  135.2 1.5 fusion.114
  138.1 1.5 fusion.114
  141.1 1.5 fusion.114
  144.1 1.5 fusion.114
  145.7 1.7 fusion.33
  147.8 19.2 %all_to_all.8 = bf16[8,256,128]{2,0,1:T(8,128)(2,1)S(1)} all-to-all(bf16[8,256,128]{2,0,1:T(8,128)(2,1)S(1)} %copy.76), channel_id=1, replica_groups=mesh['gx'=8,'gy'=4] {'gx','gy'}, dimensions={1} | all-to-all | bytes 1048576 | tf_op jit(solution)/shard_map/all_to_all | solution.py:92
  169.7 70.6 %all_gather.11 = bf16[256,256,4]{0,2,1:T(4,128)(2,1)S(1)} all-gather(bf16[256,8,4]{0,2,1:T(4,128)(2,1)S(1)} %convolution_convert_fusion), channel_id=1, replica_groups=mesh['gx'=8,'gy'=4] {'gx','gy'}, dimensions={1}, use_global_device_ids=true | all-gather | bytes 540672 | tf_op jit(solution)/shard_map/all_gather | solution.py:110
  240.9 2.5 fusion.99
  244.6 2.1 copy.84
  248.9 28.9 %while.21 = (s32[]{:T(128)}, f32[8,256,128]{2,1,0:T(8,128)}, bf16[8,256,4,32]{1,3,2,0:T(8,128)(2,1)}, bf16[8,256,4,32]{1,3,2,0:T(8,128)(2,1)}, bf16[8,256,4,32]{...) while((s32[]{:T(128)}, f32[8,256,128]{2,1,0:T(8,128)}, ...), condition=%wide.region_11.12_spmd, body=%wide.region_8.11_spmd.sunk | while | flops 119535616 | bytes 5069909 | solution.py:108
  250.3 1.5 fusion.119
  257.5 1.5 fusion.119
  268.3 1.5 fusion.119
  277.8 2.0 fusion.34
  280.1 15.8 %all_to_all.9 = bf16[256,8,128]{2,1,0:T(8,128)(2,1)S(1)} all-to-all(bf16[256,8,128]{2,1,0:T(8,128)(2,1)S(1)} %copy.89), channel_id=1, replica_groups=mesh['gx'=8,'gy'=4] {'gx','gy'}, dimensions={0} | all-to-all | bytes 1048576 | tf_op jit(solution)/shard_map/all_to_all | solution.py:112
  298.0 2.1 fusion.32
  (147 shorter events, 52.5 us)
Async XLA Ops:
  0.0 3.0 %copy-start = (bf16[128,512]{1,0:T(8,128)(2,1)S(1)}, bf16[128,512]{1,0:T(8,128)(2,1)}, u32[]{:S(2)}) copy-start(bf16[128,512]{1,0:T(8,128)(2,1)} %param.23) | copy-start | bytes 393220
  6.7 2.7 copy-start.1
  6.7 2.7 copy-start.3
  6.7 2.7 copy-start.9
  7.2 77.5 %copy-start.11 = (s32[8]{0:T(128)S(1)}, s32[8]{0:T(128)}, u32[]{:S(2)}) copy-start(s32[8]{0:T(128)} %param.21) | copy-start | bytes 100
  121.8 23.9 %copy-start.12 = (f32[128]{0:T(128)S(1)}, f32[128]{0:T(128)}, u32[]{:S(2)}) copy-start(f32[128]{0:T(128)} %param.24) | copy-start | bytes 1540
  147.4 21.6 %copy-start.4 = (f32[128]{0:T(128)S(1)}, f32[128]{0:T(128)}, u32[]{:S(2)}) copy-start(f32[128]{0:T(128)} %param.27) | copy-start | bytes 1540
  147.4 21.6 %copy-start.10 = (bf16[128,4]{0,1:T(4,128)(2,1)S(1)}, bf16[128,4]{0,1:T(4,128)(2,1)}, u32[]{:S(2)}) copy-start(bf16[128,4]{0,1:T(4,128)(2,1)} %param.30) | copy-start | bytes 3076
  167.5 73.3 %copy-start.2 = (bf16[128,512]{1,0:T(8,128)(2,1)S(1)}, bf16[128,512]{1,0:T(8,128)(2,1)}, u32[]{:S(2)}) copy-start(bf16[128,512]{1,0:T(8,128)(2,1)} %param.28) | copy-start | bytes 393220
  248.9 28.9 %copy-start.7 = (bf16[128,128]{1,0:T(8,128)(2,1)S(1)}, bf16[128,128]{1,0:T(8,128)(2,1)}, u32[]{:S(2)}) copy-start(bf16[128,128]{1,0:T(8,128)(2,1)} %param.31) | copy-start | bytes 98308
  248.9 28.9 %copy-start.13 = (f32[128]{0:T(128)S(1)}, f32[128]{0:T(128)}, u32[]{:S(2)}) copy-start(f32[128]{0:T(128)} %param.29) | copy-start | bytes 1540
  279.7 18.3 %copy-start.5 = (bf16[512,128]{1,0:T(8,128)(2,1)S(1)}, bf16[512,128]{1,0:T(8,128)(2,1)}, u32[]{:S(2)}) copy-start(bf16[512,128]{1,0:T(8,128)(2,1)} %param.35) | copy-start | bytes 393220
  279.8 18.3 %copy-start.6 = (bf16[128,512]{1,0:T(8,128)(2,1)S(1)}, bf16[128,512]{1,0:T(8,128)(2,1)}, u32[]{:S(2)}) copy-start(bf16[128,512]{1,0:T(8,128)(2,1)} %param.33) | copy-start | bytes 393220
  279.8 18.3 %copy-start.8 = (f32[512]{0:T(512)S(1)}, f32[512]{0:T(512)}, u32[]{:S(2)}) copy-start(f32[512]{0:T(512)} %param.34) | copy-start | bytes 6148
  279.8 18.3 %copy-start.14 = (f32[128]{0:T(128)S(1)}, f32[128]{0:T(128)}, u32[]{:S(2)}) copy-start(f32[128]{0:T(128)} %param.32) | copy-start | bytes 1540
where the time goes:
time: 303 us; the launch traced here: 300 us
  blocking collectives  216 us (71%)
  matrix products  56.1 us (19%)
  local copies, waits for them, and re-layouts  18.3 us (6%)
  other arithmetic  8.4 us (3%)
    all_gather x1, blocking collectives, local(): lax.all_gather(local_bias, ('gx', 'gy'), axis=0, tiled=True)  73.9 us
    all_gather x1, blocking collectives, local(): lax.all_gather(local_bias, ('gx', 'gy'), axis=1, tiled=True)  70.6 us
    unnamed x1, blocking collectives  36.8 us
    dot_general x16, matrix products, attend_block(): jnp.einsum('hjk,khd->jhd', attn_weights, values.astype(jnp.float32), prec...  23.4 us
    dot_general x16, matrix products, attend_block(): jnp.einsum('jhd,khd->hjk', query, keys, preferred_element_type=jnp.float32)  19.3 us
    all_to_all x1, blocking collectives, local(): lax.all_to_all(after_start, ('gx', 'gy'), split_axis=1, concat_axis=0, ti...  19.2 us
    all_to_all x1, blocking collectives, local(): lax.all_to_all(after_end, ('gx', 'gy'), split_axis=0, concat_axis=1, tile...  15.8 us
    dot_general x7, matrix products, project(): result = jnp.dot(flat, weight, preferred_element_type=jnp.float32)  13.4 us

commit v1 on v0

v1 whole, which is shorter than its diff:
```python
import functools
import math

import jax
import jax.numpy as jnp
from jax import lax
from jax.experimental import pallas as pl
from jax.experimental.pallas import tpu as pltpu
from jax.sharding import PartitionSpec as P

HEADS = 4
HEAD_DIM = 32
BIG = 1000000000.0
LOG2E = math.log2(math.e)
QSCALE = HEAD_DIM ** (-0.5) * LOG2E
MESH = pl.DeviceIdType.MESH
F32 = jnp.float32
BF16 = jnp.bfloat16


def nn(a, b):
    return lax.dot_general(a, b, (((1,), (0,)), ((), ())), preferred_element_type=F32)


def nt(a, b):
    return lax.dot_general(a, b, (((1,), (1,)), ((), ())), preferred_element_type=F32)


def layer_norm(x, gain):
    mean = jnp.mean(x, axis=-1, keepdims=True)
    cent = x - mean
    var = jnp.mean(cent * cent, axis=-1, keepdims=True)
    return (cent * lax.rsqrt(var + 1e-05) * gain).astype(BF16)


def bias_rows(w, r, rows, normed):
    shape = (HEADS * rows, HEADS)
    place = lax.broadcasted_iota(jnp.int32, shape, 0) == (
        lax.broadcasted_iota(jnp.int32, shape, 1) * rows + r
    )
    spread = nt(place.astype(F32).astype(BF16), w).astype(BF16)
    return nt(spread, normed)


def head_mask(shape, h):
    lane = lax.broadcasted_iota(jnp.int32, shape, 1)
    return (lane >= h * HEAD_DIM) & (lane < (h + 1) * HEAD_DIM)


def attend(q, k, v, bias_ref, start, size):
    channels = q.shape[1]
    total = None
    for h in range(HEADS):
        mask = head_mask(k.shape, h)
        zero = jnp.zeros_like(k)
        scores = nt(q, jnp.where(mask, k, zero)) + bias_ref[h, pl.ds(start, size), :]
        top = jnp.max(scores, axis=-1, keepdims=True)
        weights = jnp.exp2(scores - top).astype(BF16)
        side = jnp.concatenate(
            [jnp.where(mask, v, zero), jnp.where(mask, jnp.ones_like(v), zero)], axis=1
        )
        part = nn(weights, side)
        total = part if total is None else total + part
    return total[:, :channels] / total[:, channels:]


def kernel(
    nx,
    ny,
    tq,
    x_ref,
    mask_ref,
    g1_ref,
    w1_ref,
    gb1_ref,
    bw1_ref,
    ow1_ref,
    g2_ref,
    w2_ref,
    gb2_ref,
    bw2_ref,
    ow2_ref,
    g3_ref,
    ti_ref,
    tb_ref,
    to_ref,
    out_ref,
    a_ref,
    q_ref,
    k_ref,
    v_ref,
    bias_ref,
    kb_ref,
    zs_ref,
    send_m,
    recv_m,
    send_a,
    recv_a,
    send_b,
    recv_b,
    send_z,
    recv_z,
    recv_o,
    ssem,
    rsem,
):
    n = nx * ny
    rows, res, ch = x_ref.shape
    me = lax.axis_index("gx") * ny + lax.axis_index("gy")

    def peer_of(t):
        return lax.rem(me + t, n)

    def coords(p):
        return (p // ny, lax.rem(p, ny))

    barrier = pltpu.get_barrier_semaphore()

    @pl.loop(1, n)
    def _(t):
        pl.semaphore_signal(barrier, inc=1, device_id=coords(peer_of(t)), device_id_type=MESH)

    def share(kind, src, dst, p):
        return pltpu.make_async_remote_copy(
            src_ref=src,
            dst_ref=dst.at[me],
            send_sem=ssem.at[kind, p],
            recv_sem=rsem.at[kind, me],
            device_id=coords(p),
            device_id_type=MESH,
        )

    def arrived(kind, src, dst, p):
        return pltpu.make_async_remote_copy(
            src_ref=src,
            dst_ref=dst.at[p],
            send_sem=ssem.at[kind, p],
            recv_sem=rsem.at[kind, p],
            device_id=coords(p),
            device_id_type=MESH,
        )

    def norm_row(r, acc):
        normed = layer_norm(x_ref[r].astype(F32), g1_ref[...])
        a_ref[r] = normed
        return acc + bias_rows(bw1_ref[...], r, rows, normed)

    acc = lax.fori_loop(0, rows, norm_row, jnp.zeros((HEADS * rows, res), F32))
    send_a[...] = acc.astype(BF16)
    lane = lax.broadcasted_iota(jnp.int32, (8, 128), 0) * 128 + lax.broadcasted_iota(
        jnp.int32, (8, 128), 1
    )
    vec = jnp.zeros((8, 128), F32)
    for t in range(rows):
        vec = jnp.where(lane == me * rows + t, mask_ref[t].astype(F32), vec)
    send_m[...] = vec

    pl.semaphore_wait(barrier, n - 1)

    @pl.loop(1, n)
    def _(t):
        p = peer_of(t)
        share(0, send_m, recv_m, p).start()
        share(1, send_a, recv_a, p).start()

    recv_m[me] = send_m[...]
    recv_a[me] = send_a[...]

    def project_row(r, carry):
        p = nn(a_ref[r], w1_ref[:, : 3 * ch])
        q_ref[r] = (p[:, :ch] * QSCALE).astype(BF16)
        k_ref[r] = p[:, ch : 2 * ch].astype(BF16)
        v_ref[r] = p[:, 2 * ch :].astype(BF16)
        return carry

    lax.fori_loop(0, rows, project_row, 0)

    @pl.loop(1, n)
    def _(t):
        p = peer_of(t)
        arrived(0, send_m, recv_m, p).wait()
        arrived(1, send_a, recv_a, p).wait()

    masks = jnp.sum(recv_m[...], axis=0)
    key_mask = jnp.concatenate([masks[t : t + 1, :] for t in range(res // 128)], axis=1)
    kb_ref[...] = (key_mask - 1.0) * BIG

    def start_bias(d, carry):
        block = (recv_a[d].astype(F32) + kb_ref[...]) * LOG2E
        for h in range(HEADS):
            bias_ref[h, pl.ds(pl.multiple_of(d * rows, rows), rows), :] = block[
                h * rows : (h + 1) * rows
            ]
        return carry

    lax.fori_loop(0, n, start_bias, 0)

    def start_row(r, acc):
        pieces = []
        for c in range(res // tq):
            lo = c * tq
            o = attend(q_ref[r, lo : lo + tq, :], k_ref[r], v_ref[r], bias_ref, lo, tq)
            gl = nn(a_ref[r, lo : lo + tq, :], w1_ref[:, 3 * ch :])
            gated = (o * jax.nn.sigmoid(gl + gb1_ref[...])).astype(BF16)
            z1 = x_ref[r, lo : lo + tq, :].astype(F32) + nn(gated, ow1_ref[...])
            z1 = z1.astype(BF16).astype(F32)
            zs_ref[lo // rows : (lo + tq) // rows, pl.ds(r, rows, stride=rows), :] = z1.reshape(
                tq // rows, rows, ch
            )
            pieces.append(layer_norm(z1, g2_ref[...]))
        normed = pieces[0] if len(pieces) == 1 else jnp.concatenate(pieces, axis=0)
        return acc + bias_rows(bw2_ref[...], r, rows, normed)

    acc = lax.fori_loop(0, rows, start_row, jnp.zeros((HEADS * rows, res), F32))
    send_b[...] = acc.astype(BF16)
    send_z[...] = zs_ref[...].astype(BF16)

    @pl.loop(1, n)
    def _(t):
        p = peer_of(t)
        share(2, send_b, recv_b, p).start()
        share(3, send_z.at[p], recv_z, p).start()

    recv_b[me] = send_b[...]
    recv_z[me] = send_z[me]

    @pl.loop(1, n)
    def _(t):
        p = peer_of(t)
        arrived(2, send_b, recv_b, p).wait()
        arrived(3, send_z.at[p], recv_z, p).wait()

    zs_ref[...] = recv_z[...].astype(F32)
    kd = 128 // rows
    for t in range(res // 128):
        block = recv_b[t * kd : (t + 1) * kd].astype(F32)
        for h in range(HEADS):
            turned = block[:, h * rows : (h + 1) * rows, :].reshape(128, res).T
            bias_ref[h, :, t * 128 : (t + 1) * 128] = (
                turned + kb_ref[:, t * 128 : (t + 1) * 128]
            ) * LOG2E

    def end_col(c, carry):
        own = pl.ds(pl.multiple_of(c * rows, rows), rows)
        normed = layer_norm(zs_ref[:, own, :].reshape(res, ch), g2_ref[...])
        p = nn(normed, w2_ref[...])
        q = (p[:, :ch] * QSCALE).astype(BF16)
        k = p[:, ch : 2 * ch].astype(BF16)
        v = p[:, 2 * ch : 3 * ch].astype(BF16)
        gate = jax.nn.sigmoid(p[:, 3 * ch :] + gb2_ref[...])
        for s in range(res // tq):
            lo = s * tq
            o = attend(q[lo : lo + tq], k, v, bias_ref, lo, tq)
            gated = (o * gate[lo : lo + tq]).astype(BF16)
            span = slice(lo // rows, (lo + tq) // rows)
            z2 = zs_ref[span, own, :].reshape(tq, ch) + nn(gated, ow2_ref[...])
            z2 = z2.astype(BF16).astype(F32)
            hid = nn(layer_norm(z2, g3_ref[...]), ti_ref[...]) + tb_ref[...]
            hid = jnp.maximum(hid, 0.0).astype(BF16)
            z3 = z2 + nn(hid, to_ref[...])
            zs_ref[span, own, :] = z3.reshape(tq // rows, rows, ch)
        return carry

    lax.fori_loop(0, rows, end_col, 0)
    send_z[...] = zs_ref[...].astype(BF16)

    @pl.loop(1, n)
    def _(t):
        p = peer_of(t)
        share(4, send_z.at[p], recv_o, p).start()

    recv_o[me] = send_z[me]

    @pl.loop(1, n)
    def _(t):
        p = peer_of(t)
        arrived(4, send_z.at[p], recv_o, p).wait()

    zs_ref[...] = recv_o[...].astype(F32)

    def out_row(r, carry):
        out_ref[r] = zs_ref[:, pl.ds(r, rows, stride=rows), :].reshape(res, ch).astype(BF16)
        return carry

    lax.fori_loop(0, rows, out_row, 0)


def solution(mesh):
    nx, ny = mesh.shape["gx"], mesh.shape["gy"]
    n = nx * ny

    def local(x, mask, g1, w1, gb1, bw1, ow1, g2, w2, gb2, bw2, ow2, g3, ti, tb, to):
        rows, res, ch = x.shape
        tq = min(res, 256)
        vmem = pl.BlockSpec(memory_space=pltpu.VMEM)
        row = lambda t: t.reshape(1, -1)
        return pl.pallas_call(
            functools.partial(kernel, nx, ny, tq),
            out_shape=jax.ShapeDtypeStruct(x.shape, x.dtype),
            in_specs=[vmem, pl.BlockSpec(memory_space=pltpu.SMEM)] + [vmem] * 14,
            out_specs=vmem,
            scratch_shapes=[
                pltpu.VMEM((rows, res, ch), BF16),
                pltpu.VMEM((rows, res, ch), BF16),
                pltpu.VMEM((rows, res, ch), BF16),
                pltpu.VMEM((rows, res, ch), BF16),
                pltpu.VMEM((HEADS, res, res), F32),
                pltpu.VMEM((1, res), F32),
                pltpu.VMEM((n, rows * rows, ch), F32),
                pltpu.VMEM((8, 128), F32),
                pltpu.VMEM((n, 8, 128), F32),
                pltpu.VMEM((HEADS * rows, res), BF16),
                pltpu.VMEM((n, HEADS * rows, res), BF16),
                pltpu.VMEM((HEADS * rows, res), BF16),
                pltpu.VMEM((n, HEADS * rows, res), BF16),
                pltpu.VMEM((n, rows * rows, ch), BF16),
                pltpu.VMEM((n, rows * rows, ch), BF16),
                pltpu.VMEM((n, rows * rows, ch), BF16),
                pltpu.SemaphoreType.DMA((5, n)),
                pltpu.SemaphoreType.DMA((5, n)),
            ],
            compiler_params=pltpu.CompilerParams(
                collective_id=0, has_side_effects=True, vmem_limit_bytes=66 * 1000 * 1000
            ),
        )(
            x, mask, row(g1), w1, row(gb1), bw1, ow1, row(g2), w2, row(gb2), bw2, ow2,
            row(g3), ti, row(tb), to,
        )

    placed = (P(("gx", "gy"), None, None), P(("gx", "gy"))) + (P(),) * 14
    return jax.shard_map(
        local, mesh=mesh, in_specs=placed, out_specs=P(("gx", "gy"), None, None), check_vma=False
    )
```

time: 303 us -> 93.7 us (0.31)
  blocking collectives: 216 us -> 0 us
  Pallas kernels: 0 us -> 89.4 us
  matrix products: 56.1 us -> 0 us
  local copies, waits for them, and re-layouts: 18.3 us -> 4.01 us
  other arithmetic: 8.4 us -> 0 us
    all_gather x2 -> x0, blocking collectives: 145 us -> none  [the longest x1 73.9 us: local(): lax.all_gather(local_bias, ('gx', 'gy'), axis=0, tiled=True)]
    pallas_call x0 -> x1, Pallas kernels: none -> 89.4 us  [local(): pl.pallas_call(functools.partial(kernel, nx, ny, tq), out_shape=jax.Shape...]
    dot_general x39 -> x0, matrix products: 56.1 us -> none  [the longest x16 23.4 us: attend_block(): jnp.einsum('hjk,khd->jhd', attn_weights, values.astype(jnp.float32), prec...]
    unnamed x1 -> x0, blocking collectives: 36.8 us -> none
    all_to_all x2 -> x0, blocking collectives: 35 us -> none  [the longest x1 19.2 us: local(): lax.all_to_all(after_start, ('gx', 'gy'), split_axis=1, concat_axis=0, ti...]
    reduce_sum x22 -> x0, other arithmetic: 7.57 us -> none  [the longest x3 2.99 us: layer_norm(): row_var = jnp.mean(jnp.square(widened - row_mean), axis=-1, keepdims=True)]
    slice x8 -> x0, local copies, waits for them, and re-layouts: 7.14 us -> none  [the longest x2 3.06 us: projections(): values = split_heads(projected[..., 2 * channels:3 * channels])]
    dynamic_update_slice x32 -> x0, local copies, waits for them, and re-layouts: 6.85 us -> none  [start_block(): return lax.map(per_row, (query_part, keys, values))]
where the time goes in v1:
time: 93.7 us; the launch traced here: 93.4 us
  Pallas kernels  89.4 us (95%)
  local copies, waits for them, and re-layouts  4.01 us (4%)
    pallas_call x1, Pallas kernels, local(): pl.pallas_call(functools.partial(kernel, nx, ny, tq), out_shape=jax.Shape...  89.4 us
    unnamed x7, local copies, waits for them, and re-layouts  4.01 us

profile of v1, /device:TPU:0, one launch (start us, length us, event | category | flops | bytes accessed | tf_op | source)
XLA Modules:
  0.0 93.4 jit_solution(4441461109806100405)
XLA Ops:
  0.0 0.0 copy-start
  0.0 0.7 copy-done
  0.7 0.0 copy-start.1
  0.7 0.7 copy.17.bw1_ref
  1.4 0.0 copy-done.1
  1.4 0.7 copy.18.bw2_ref
  2.1 89.4 %shard_map.154 = bf16[8,256,128]{2,1,0:T(8,128)(2,1)} custom-call(bf16[8,256,128]{2,1,0:T(8,128)(2,1)} %x_ref.1, s32[8]{0:T(128)} %mask_ref.1, f32[1,128]{1,0:T(1,128)} %bitcast.7, bf16[128,512]{1,0:T(8,128)(2,1)} %w1_ref.1, f32[1,128]{1,0:T(1,128)} %bitcast.8, bf16[128,4]{1,0:T(8,128)(2,1)} %copy.17.bw1_ref, bf16[128,128]{1,0:T(8,128)(2,1)} %ow1_ref.1, ...), custom_call_target="tpu_custom_call" | custom-call | tf_op jit(solution)/shard_map/pallas_call | solution.py:297
  91.5 1.9 %copy.20 = bf16[8,256,128]{2,1,0:T(8,128)(2,1)} copy(bf16[8,256,128]{2,1,0:T(8,128)(2,1)} %shard_map.154) | data formatting | bytes 1048576
Async XLA Ops:
  0.0 0.7 copy-start
  0.7 0.7 copy-start.1

commit v2 on v1

v2 whole, which is shorter than its diff:
```python
import functools
import math

import jax
import jax.numpy as jnp
from jax import lax
from jax.experimental import pallas as pl
from jax.experimental.pallas import tpu as pltpu
from jax.sharding import PartitionSpec as P

HEADS = 4
HEAD_DIM = 32
BIG = 1000000000.0
LOG2E = math.log2(math.e)
QSCALE = HEAD_DIM ** (-0.5) * LOG2E
MESH = pl.DeviceIdType.MESH
F32 = jnp.float32
BF16 = jnp.bfloat16


def nn(a, b):
    return lax.dot_general(a, b, (((1,), (0,)), ((), ())), preferred_element_type=F32)


def nt(a, b):
    return lax.dot_general(a, b, (((1,), (1,)), ((), ())), preferred_element_type=F32)


def layer_norm(x, gain):
    mean = jnp.mean(x, axis=-1, keepdims=True)
    cent = x - mean
    var = jnp.mean(cent * cent, axis=-1, keepdims=True)
    return (cent * lax.rsqrt(var + 1e-05) * gain).astype(BF16)


def bias_rows(w, r, rows, normed):
    shape = (HEADS * rows, HEADS)
    place = lax.broadcasted_iota(jnp.int32, shape, 0) == (
        lax.broadcasted_iota(jnp.int32, shape, 1) * rows + r
    )
    spread = nn(place.astype(F32).astype(BF16), w).astype(BF16)
    return nt(spread, normed)


def head_mask(shape, h):
    lane = lax.broadcasted_iota(jnp.int32, shape, 1)
    return (lane >= h * HEAD_DIM) & (lane < (h + 1) * HEAD_DIM)


def attend(q, k, v, bias_ref, start, size):
    channels = q.shape[1]
    total = None
    for h in range(HEADS):
        mask = head_mask(k.shape, h)
        zero = jnp.zeros_like(k)
        scores = nt(q, jnp.where(mask, k, zero)) + bias_ref[h, pl.ds(start, size), :]
        top = jnp.max(scores, axis=-1, keepdims=True)
        weights = jnp.exp2(scores - top).astype(BF16)
        side = jnp.concatenate(
            [jnp.where(mask, v, zero), jnp.where(mask, jnp.ones_like(v), zero)], axis=1
        )
        part = nn(weights, side)
        total = part if total is None else total + part
    return total[:, :channels] / total[:, channels:]


def kernel(
    nx,
    ny,
    tq,
    x_ref,
    mask_ref,
    g1_ref,
    w1_ref,
    gb1_ref,
    bw1_ref,
    ow1_ref,
    g2_ref,
    w2_ref,
    gb2_ref,
    bw2_ref,
    ow2_ref,
    g3_ref,
    ti_ref,
    tb_ref,
    to_ref,
    out_ref,
    a_ref,
    q_ref,
    k_ref,
    v_ref,
    bias_ref,
    kb_ref,
    zs_ref,
    send_m,
    recv_m,
    recv_a,
    recv_b,
    send_z,
    recv_z,
    recv_o,
    ssem,
    rsem,
    fsem,
    lsem,
):
    n = nx * ny
    rows, res, ch = x_ref.shape
    me = lax.axis_index("gx") * ny + lax.axis_index("gy")

    def peer_of(t):
        return lax.rem(me + t, n)

    def coords(p):
        return (p // ny, lax.rem(p, ny))

    barrier = pltpu.get_barrier_semaphore()

    @pl.loop(1, n)
    def _(t):
        pl.semaphore_signal(barrier, inc=1, device_id=coords(peer_of(t)), device_id_type=MESH)

    def move(kind, src, dst, p, slot):
        return pltpu.make_async_remote_copy(
            src_ref=src,
            dst_ref=dst,
            send_sem=ssem.at[kind, slot],
            recv_sem=rsem.at[kind, slot],
            device_id=coords(p),
            device_id_type=MESH,
        )

    def share(kind, src, dst, p):
        return pltpu.make_async_remote_copy(
            src_ref=src,
            dst_ref=dst,
            send_sem=ssem.at[kind, p],
            recv_sem=rsem.at[kind, me],
            device_id=coords(p),
            device_id_type=MESH,
        )

    gx, gy = lax.axis_index("gx"), lax.axis_index("gy")
    core = lax.rem(gx, 2)
    half = nx // 2
    partner = (gx + 1 - 2 * core) * ny + gy

    def line_peer(t):
        return gx * ny + lax.rem(gy + t, ny)

    def plane_peer(t):
        return (lax.rem(gx // 2 + t, half) * 2 + core) * ny + gy

    def relay(kind, buf, t, s):
        @pl.loop(1, half)
        def _(u):
            q = plane_peer(u)
            pltpu.make_async_remote_copy(
                src_ref=buf.at[s],
                dst_ref=buf.at[s],
                send_sem=fsem.at[kind, t, u],
                recv_sem=rsem.at[kind, s],
                device_id=coords(q),
                device_id_type=MESH,
            ).start()

        hand(kind, buf, s).start()

    def hand(kind, buf, s):
        return move(kind, buf.at[s], buf.at[s], partner, s)

    def gather_start(kind, buf):
        @pl.loop(1, ny)
        def _(t):
            p = line_peer(t)
            pltpu.make_async_remote_copy(
                src_ref=buf.at[me],
                dst_ref=buf.at[me],
                send_sem=lsem.at[kind, t],
                recv_sem=rsem.at[kind, me],
                device_id=coords(p),
                device_id_type=MESH,
            ).start()

        relay(kind, buf, 0, me)

    def gather_finish(kind, buf):
        @pl.loop(1, ny)
        def _(t):
            p = line_peer(t)
            move(kind, buf.at[p], buf.at[p], p, p).wait_recv()
            relay(kind, buf, t, p)

        @pl.loop(0, ny)
        def _(t):
            @pl.loop(1, half)
            def _(u):
                s = plane_peer(u) - gy + lax.rem(gy + t, ny)
                move(kind, buf.at[s], buf.at[s], partner, s).wait_recv()
                hand(kind, buf, s).start()

        @pl.loop(0, ny)
        def _(t):
            @pl.loop(0, half)
            def _(u):
                s = plane_peer(u) - gy + lax.rem(gy + t, ny)
                o = s + (1 - 2 * core) * ny
                move(kind, buf.at[o], buf.at[o], partner, o).wait_recv()
                hand(kind, buf, s).wait_send()

            @pl.loop(1, half)
            def _(u):
                pltpu.make_async_remote_copy(
                    src_ref=buf.at[me],
                    dst_ref=buf.at[me],
                    send_sem=fsem.at[kind, t, u],
                    recv_sem=rsem.at[kind, me],
                    device_id=coords(partner),
                    device_id_type=MESH,
                ).wait_send()

        @pl.loop(1, ny)
        def _(t):
            pltpu.make_async_remote_copy(
                src_ref=buf.at[me],
                dst_ref=buf.at[me],
                send_sem=lsem.at[kind, t],
                recv_sem=rsem.at[kind, me],
                device_id=coords(partner),
                device_id_type=MESH,
            ).wait_send()

    def spread_pair(kind, src, dst, g):
        part = pl.ds(pl.multiple_of(g * 2 * rows, 2 * rows), 2 * rows)

        @pl.loop(1, n)
        def _(t):
            p = peer_of(t)
            share(kind, src.at[p, part], dst.at[me, part], p).start()

        dst[me, part] = src[me, part]

    def spread_finish(kind, src, dst):
        @pl.loop(1, n)
        def _(t):
            p = peer_of(t)
            move(kind, src.at[p], dst.at[p], p, p).wait()

    def norm_row(r, acc):
        normed = layer_norm(x_ref[r].astype(F32), g1_ref[...])
        a_ref[r] = normed
        return acc + bias_rows(bw1_ref[...], r, rows, normed)

    acc = lax.fori_loop(0, rows, norm_row, jnp.zeros((HEADS * rows, res), F32))
    recv_a[me] = acc.astype(BF16)
    lane = lax.broadcasted_iota(jnp.int32, (1, 128), 1)
    vec = jnp.zeros((1, 128), F32)
    for t in range(rows):
        vec = jnp.where(lane == lax.rem(me * rows, 128) + t, mask_ref[t].astype(F32), vec)
    send_m[...] = vec

    pl.semaphore_wait(barrier, n - 1)

    gather_start(0, recv_a)

    @pl.loop(1, n)
    def _(t):
        p = peer_of(t)
        share(2, send_m, recv_m.at[me], p).start()

    recv_m[me] = send_m[...]

    def project_row(r, carry):
        p = nn(a_ref[r], w1_ref[:, : 3 * ch])
        q_ref[r] = (p[:, :ch] * QSCALE).astype(BF16)
        k_ref[r] = p[:, ch : 2 * ch].astype(BF16)
        v_ref[r] = p[:, 2 * ch :].astype(BF16)
        return carry

    lax.fori_loop(0, rows, project_row, 0)

    gather_finish(0, recv_a)

    @pl.loop(1, n)
    def _(t):
        p = peer_of(t)
        move(2, send_m, recv_m.at[p], p, p).wait()

    kd = 128 // rows
    key_mask = jnp.concatenate(
        [jnp.sum(recv_m[t * kd : (t + 1) * kd], axis=0) for t in range(res // 128)], axis=1
    )
    kb_ref[...] = (key_mask - 1.0) * BIG

    def start_bias(d, carry):
        block = (recv_a[d].astype(F32) + kb_ref[...]) * LOG2E
        for h in range(HEADS):
            bias_ref[h, pl.ds(pl.multiple_of(d * rows, rows), rows), :] = block[
                h * rows : (h + 1) * rows
            ]
        return carry

    lax.fori_loop(0, n, start_bias, 0)

    def start_pair(g, acc):
        found = []
        for c in range(res // tq):
            lo = c * tq
            blocks, rise = [], None
            for e in range(2):
                r = 2 * g + e
                o = attend(q_ref[r, lo : lo + tq, :], k_ref[r], v_ref[r], bias_ref, lo, tq)
                gl = nn(a_ref[r, lo : lo + tq, :], w1_ref[:, 3 * ch :])
                gated = (o * jax.nn.sigmoid(gl + gb1_ref[...])).astype(BF16)
                z1 = x_ref[r, lo : lo + tq, :].astype(F32) + nn(gated, ow1_ref[...])
                z1 = z1.astype(BF16).astype(F32)
                blocks.append(z1.reshape(tq // rows, rows, ch))
                part = bias_rows(bw2_ref[...], r, rows, layer_norm(z1, g2_ref[...]))
                rise = part if rise is None else rise + part
            send_z[
                lo // rows : (lo + tq) // rows,
                pl.ds(pl.multiple_of(g * 2 * rows, 2 * rows), 2 * rows),
                :,
            ] = jnp.concatenate(blocks, axis=1).astype(BF16)
            found.append(rise)
        spread_pair(3, send_z, recv_z, g)
        return acc + (found[0] if len(found) == 1 else jnp.concatenate(found, axis=1))

    acc = lax.fori_loop(0, rows // 2, start_pair, jnp.zeros((HEADS * rows, res), F32))
    recv_b[me] = acc.astype(BF16)
    gather_start(1, recv_b)
    gather_finish(1, recv_b)
    spread_finish(3, send_z, recv_z)

    zs_ref[...] = recv_z[...].astype(F32)
    for t in range(res // 128):
        block = recv_b[t * kd : (t + 1) * kd].astype(F32)
        for h in range(HEADS):
            turned = block[:, h * rows : (h + 1) * rows, :].reshape(128, res).T
            bias_ref[h, :, t * 128 : (t + 1) * 128] = (
                turned + kb_ref[:, t * 128 : (t + 1) * 128]
            ) * LOG2E

    def end_pair(g, carry):
        ready = []
        for e in range(2):
            z1 = zs_ref[:, pl.ds(2 * g + e, rows, stride=rows), :].reshape(res, ch)
            p = nn(layer_norm(z1, g2_ref[...]), w2_ref[...])
            q = (p[:, :ch] * QSCALE).astype(BF16)
            k = p[:, ch : 2 * ch].astype(BF16)
            v = p[:, 2 * ch : 3 * ch].astype(BF16)
            gate = jax.nn.sigmoid(p[:, 3 * ch :] + gb2_ref[...])
            ready.append((z1, q, k, v, gate))
        for s in range(res // tq):
            lo = s * tq
            blocks = []
            for z1, q, k, v, gate in ready:
                o = attend(q[lo : lo + tq], k, v, bias_ref, lo, tq)
                gated = (o * gate[lo : lo + tq]).astype(BF16)
                z2 = z1[lo : lo + tq] + nn(gated, ow2_ref[...])
                z2 = z2.astype(BF16).astype(F32)
                hid = nn(layer_norm(z2, g3_ref[...]), ti_ref[...]) + tb_ref[...]
                hid = jnp.maximum(hid, 0.0).astype(BF16)
                z3 = z2 + nn(hid, to_ref[...])
                blocks.append(z3.reshape(tq // rows, rows, ch))
            send_z[
                lo // rows : (lo + tq) // rows,
                pl.ds(pl.multiple_of(g * 2 * rows, 2 * rows), 2 * rows),
                :,
            ] = jnp.concatenate(blocks, axis=1).astype(BF16)
        spread_pair(4, send_z, recv_o, g)
        return carry

    lax.fori_loop(0, rows // 2, end_pair, 0)
    spread_finish(4, send_z, recv_o)

    zs_ref[...] = recv_o[...].astype(F32)

    def out_row(r, carry):
        out_ref[r] = zs_ref[:, pl.ds(r, rows, stride=rows), :].reshape(res, ch).astype(BF16)
        return carry

    lax.fori_loop(0, rows, out_row, 0)


def solution(mesh):
    nx, ny = mesh.shape["gx"], mesh.shape["gy"]
    n = nx * ny

    def local(x, mask, g1, w1, gb1, bw1, ow1, g2, w2, gb2, bw2, ow2, g3, ti, tb, to):
        rows, res, ch = x.shape
        tq = 256 if res <= 256 else 128
        vmem = pl.BlockSpec(memory_space=pltpu.VMEM)
        row = lambda t: t.reshape(1, -1)
        return pl.pallas_call(
            functools.partial(kernel, nx, ny, tq),
            out_shape=jax.ShapeDtypeStruct(x.shape, x.dtype),
            in_specs=[vmem, pl.BlockSpec(memory_space=pltpu.SMEM)] + [vmem] * 14,
            out_specs=vmem,
            scratch_shapes=[
                pltpu.VMEM((rows, res, ch), BF16),
                pltpu.VMEM((rows, res, ch), BF16),
                pltpu.VMEM((rows, res, ch), BF16),
                pltpu.VMEM((rows, res, ch), BF16),
                pltpu.VMEM((HEADS, res, res), F32),
                pltpu.VMEM((1, res), F32),
                pltpu.VMEM((n, rows * rows, ch), F32),
                pltpu.VMEM((1, 128), F32),
                pltpu.VMEM((n, 1, 128), F32),
                pltpu.VMEM((n, HEADS * rows, res), BF16),
                pltpu.VMEM((n, HEADS * rows, res), BF16),
                pltpu.VMEM((n, rows * rows, ch), BF16),
                pltpu.VMEM((n, rows * rows, ch), BF16),
                pltpu.VMEM((n, rows * rows, ch), BF16),
                pltpu.SemaphoreType.DMA((5, n)),
                pltpu.SemaphoreType.DMA((5, n)),
                pltpu.SemaphoreType.DMA((2, ny, nx // 2)),
                pltpu.SemaphoreType.DMA((2, ny)),
            ],
            compiler_params=pltpu.CompilerParams(
                collective_id=0, has_side_effects=True, vmem_limit_bytes=66 * 1000 * 1000
            ),
        )(
            x, mask, row(g1), w1, row(gb1), bw1.T, ow1, row(g2), w2, row(gb2), bw2.T, ow2,
            row(g3), ti, row(tb), to,
        )

    placed = (P(("gx", "gy"), None, None), P(("gx", "gy"))) + (P(),) * 14
    return jax.shard_map(
        local, mesh=mesh, in_specs=placed, out_specs=P(("gx", "gy"), None, None), check_vma=False
    )
```

time: 93.7 us -> 64.7 us (0.69)
  Pallas kernels: 89.4 us -> 62.6 us
  local copies, waits for them, and re-layouts: 4.01 us -> 1.87 us
    pallas_call x1, Pallas kernels: 89.4 us -> 62.6 us  [local(): pl.pallas_call(functools.partial(kernel, nx, ny, tq), out_shape=jax.Shape...]
    unnamed x7 -> x1, local copies, waits for them, and re-layouts: 4.01 us -> 1.87 us
where the time goes in v2:
time: 64.7 us; the launch traced here: 64.5 us
  Pallas kernels  62.6 us (97%)
  local copies, waits for them, and re-layouts  1.87 us (3%)
    pallas_call x1, Pallas kernels, local(): pl.pallas_call(functools.partial(kernel, nx, ny, tq), out_shape=jax.Shape...  62.6 us
    unnamed x1, local copies, waits for them, and re-layouts  1.87 us

profile of v2, /device:TPU:0, one launch (start us, length us, event | category | flops | bytes accessed | tf_op | source)
XLA Modules:
  0.0 64.5 jit_solution(1786545071548920381)
XLA Ops:
  0.0 62.6 %shard_map.154 = bf16[8,256,128]{2,1,0:T(8,128)(2,1)} custom-call(bf16[8,256,128]{2,1,0:T(8,128)(2,1)} %x_ref.1, s32[8]{0:T(128)} %mask_ref.1, f32[1,128]{1,0:T(1,128)} %bitcast.11, bf16[128,512]{1,0:T(8,128)(2,1)} %w1_ref.1, f32[1,128]{1,0:T(1,128)} %bitcast.12, bf16[4,128]{1,0:T(4,128)(2,1)} %bitcast.9, bf16[128,128]{1,0:T(8,128)(2,1)} %ow1_ref.1, ...), custom_call_target="tpu_custom_call" | custom-call | tf_op jit(solution)/shard_map/pallas_call | solution.py:395
  62.6 1.9 %copy.18 = bf16[8,256,128]{2,1,0:T(8,128)(2,1)} copy(bf16[8,256,128]{2,1,0:T(8,128)(2,1)} %shard_map.154) | data formatting | bytes 1048576

commit v3 on v2

--- a/solution.py
+++ b/solution.py
@@ -302,6 +302,8 @@
 
     lax.fori_loop(0, n, start_bias, 0)
 
+    early = rows // 4
+
     def start_pair(g, acc):
         found = []
         for c in range(res // tq):
@@ -323,12 +325,21 @@
                 :,
             ] = jnp.concatenate(blocks, axis=1).astype(BF16)
             found.append(rise)
-        spread_pair(3, send_z, recv_z, g)
+
+        @pl.when(g < early)
+        def _():
+            spread_pair(3, send_z, recv_z, g)
+
         return acc + (found[0] if len(found) == 1 else jnp.concatenate(found, axis=1))
 
     acc = lax.fori_loop(0, rows // 2, start_pair, jnp.zeros((HEADS * rows, res), F32))
     recv_b[me] = acc.astype(BF16)
     gather_start(1, recv_b)
+
+    @pl.loop(early, rows // 2)
+    def _(g):
+        spread_pair(3, send_z, recv_z, g)
+
     gather_finish(1, recv_b)
     spread_finish(3, send_z, recv_z)
 

time: 64.7 us -> 61.5 us (0.951)
  Pallas kernels: 62.6 us -> 59.4 us
    pallas_call x1, Pallas kernels: 62.6 us -> 59.4 us  [local(): pl.pallas_call(functools.partial(kernel, nx, ny, tq), out_shape=jax.Shape...]
where the time goes in v3:
time: 61.5 us; the launch traced here: 61.3 us
  Pallas kernels  59.4 us (97%)
  local copies, waits for them, and re-layouts  1.87 us (3%)
    pallas_call x1, Pallas kernels, local(): pl.pallas_call(functools.partial(kernel, nx, ny, tq), out_shape=jax.Shape...  59.4 us
    unnamed x1, local copies, waits for them, and re-layouts  1.87 us

profile of v3, /device:TPU:0, one launch (start us, length us, event | category | flops | bytes accessed | tf_op | source)
XLA Modules:
  0.0 61.3 jit_solution(4644921294021817164)
XLA Ops:
  0.0 59.4 %shard_map.154 = bf16[8,256,128]{2,1,0:T(8,128)(2,1)} custom-call(bf16[8,256,128]{2,1,0:T(8,128)(2,1)} %x_ref.1, s32[8]{0:T(128)} %mask_ref.1, f32[1,128]{1,0:T(1,128)} %bitcast.11, bf16[128,512]{1,0:T(8,128)(2,1)} %w1_ref.1, f32[1,128]{1,0:T(1,128)} %bitcast.12, bf16[4,128]{1,0:T(4,128)(2,1)} %bitcast.9, bf16[128,128]{1,0:T(8,128)(2,1)} %ow1_ref.1, ...), custom_call_target="tpu_custom_call" | custom-call | tf_op jit(solution)/shard_map/pallas_call | solution.py:406
  59.4 1.9 %copy.18 = bf16[8,256,128]{2,1,0:T(8,128)(2,1)} copy(bf16[8,256,128]{2,1,0:T(8,128)(2,1)} %shard_map.154) | data formatting | bytes 1048576

commit v4 on v3

--- a/solution.py
+++ b/solution.py
@@ -85,15 +85,12 @@
     tb_ref,
     to_ref,
     out_ref,
-    a_ref,
     q_ref,
     k_ref,
     v_ref,
     bias_ref,
     kb_ref,
     zs_ref,
-    send_m,
-    recv_m,
     recv_a,
     recv_b,
     send_z,
@@ -114,11 +111,6 @@
     def coords(p):
         return (p // ny, lax.rem(p, ny))
 
-    barrier = pltpu.get_barrier_semaphore()
-
-    @pl.loop(1, n)
-    def _(t):
-        pl.semaphore_signal(barrier, inc=1, device_id=coords(peer_of(t)), device_id_type=MESH)
 
     def move(kind, src, dst, p, slot):
         return pltpu.make_async_remote_copy(
@@ -141,6 +133,7 @@
         )
 
     gx, gy = lax.axis_index("gx"), lax.axis_index("gy")
+    a_ref = out_ref
     core = lax.rem(gx, 2)
     half = nx // 2
     partner = (gx + 1 - 2 * core) * ny + gy
@@ -150,6 +143,17 @@
 
     def plane_peer(t):
         return (lax.rem(gx // 2 + t, half) * 2 + core) * ny + gy
+
+    barrier = pltpu.get_barrier_semaphore()
+
+    def greet(p):
+        pl.semaphore_signal(barrier, inc=1, device_id=coords(p), device_id_type=MESH)
+
+    for t in range(1, ny):
+        greet(line_peer(t))
+    for t in range(1, half):
+        greet(plane_peer(t))
+    greet(partner)
 
     def relay(kind, buf, t, s):
         @pl.loop(1, half)
@@ -252,23 +256,18 @@
         return acc + bias_rows(bw1_ref[...], r, rows, normed)
 
     acc = lax.fori_loop(0, rows, norm_row, jnp.zeros((HEADS * rows, res), F32))
-    recv_a[me] = acc.astype(BF16)
-    lane = lax.broadcasted_iota(jnp.int32, (1, 128), 1)
-    vec = jnp.zeros((1, 128), F32)
+    deep, wide = HEADS * rows, res // 128
+    for t in range(wide):
+        recv_a[me, t * deep : (t + 1) * deep, :] = acc[:, t * 128 : (t + 1) * 128].astype(BF16)
+    lane = lax.broadcasted_iota(jnp.int32, (16, 128), 1)
+    vec = jnp.zeros((16, 128), F32)
     for t in range(rows):
         vec = jnp.where(lane == lax.rem(me * rows, 128) + t, mask_ref[t].astype(F32), vec)
-    send_m[...] = vec
-
-    pl.semaphore_wait(barrier, n - 1)
+    recv_a[me, wide * deep :, :] = vec.astype(BF16)
+
+    pl.semaphore_wait(barrier, ny + half - 1)
 
     gather_start(0, recv_a)
-
-    @pl.loop(1, n)
-    def _(t):
-        p = peer_of(t)
-        share(2, send_m, recv_m.at[me], p).start()
-
-    recv_m[me] = send_m[...]
 
     def project_row(r, carry):
         p = nn(a_ref[r], w1_ref[:, : 3 * ch])
@@ -281,23 +280,23 @@
 
     gather_finish(0, recv_a)
 
-    @pl.loop(1, n)
-    def _(t):
-        p = peer_of(t)
-        move(2, send_m, recv_m.at[p], p, p).wait()
-
     kd = 128 // rows
-    key_mask = jnp.concatenate(
-        [jnp.sum(recv_m[t * kd : (t + 1) * kd], axis=0) for t in range(res // 128)], axis=1
-    )
+    masks = [
+        jnp.sum(recv_a[t * kd : (t + 1) * kd, wide * deep :, :].astype(F32), axis=0)[:1]
+        for t in range(wide)
+    ]
+    key_mask = masks[0] if wide == 1 else jnp.concatenate(masks, axis=1)
     kb_ref[...] = (key_mask - 1.0) * BIG
 
     def start_bias(d, carry):
-        block = (recv_a[d].astype(F32) + kb_ref[...]) * LOG2E
-        for h in range(HEADS):
-            bias_ref[h, pl.ds(pl.multiple_of(d * rows, rows), rows), :] = block[
-                h * rows : (h + 1) * rows
-            ]
+        for t in range(wide):
+            span = slice(t * 128, (t + 1) * 128)
+            block = recv_a[d, t * deep : (t + 1) * deep, :].astype(F32)
+            block = (block + kb_ref[:, span]) * LOG2E
+            for h in range(HEADS):
+                bias_ref[h, pl.ds(pl.multiple_of(d * rows, rows), rows), span] = block[
+                    h * rows : (h + 1) * rows
+                ]
         return carry
 
     lax.fori_loop(0, n, start_bias, 0)
@@ -412,13 +411,10 @@
                 pltpu.VMEM((rows, res, ch), BF16),
                 pltpu.VMEM((rows, res, ch), BF16),
                 pltpu.VMEM((rows, res, ch), BF16),
-                pltpu.VMEM((rows, res, ch), BF16),
                 pltpu.VMEM((HEADS, res, res), F32),
                 pltpu.VMEM((1, res), F32),
                 pltpu.VMEM((n, rows * rows, ch), F32),
-                pltpu.VMEM((1, 128), F32),
-                pltpu.VMEM((n, 1, 128), F32),
-                pltpu.VMEM((n, HEADS * rows, res), BF16),
+                pltpu.VMEM((n, HEADS * rows * (res // 128) + 16, 128), BF16),
                 pltpu.VMEM((n, HEADS * rows, res), BF16),
                 pltpu.VMEM((n, rows * rows, ch), BF16),
                 pltpu.VMEM((n, rows * rows, ch), BF16),

time: 61.5 us -> 60.6 us (0.985)
  Pallas kernels: 59.4 us -> 58.5 us
    pallas_call x1, Pallas kernels: 59.4 us -> 58.5 us  [local(): pl.pallas_call(functools.partial(kernel, nx, ny, tq), out_shape=jax.Shape...]
where the time goes in v4:
time: 60.6 us; the launch traced here: 60.4 us
  Pallas kernels  58.5 us (97%)
  local copies, waits for them, and re-layouts  1.87 us (3%)
    pallas_call x1, Pallas kernels, local(): pl.pallas_call(functools.partial(kernel, nx, ny, tq), out_shape=jax.Shape...  58.5 us
    unnamed x1, local copies, waits for them, and re-layouts  1.87 us

profile of v4, /device:TPU:0, one launch (start us, length us, event | category | flops | bytes accessed | tf_op | source)
XLA Modules:
  0.0 60.4 jit_solution(17782349983395467688)
XLA Ops:
  0.0 58.5 %shard_map.154 = bf16[8,256,128]{2,1,0:T(8,128)(2,1)} custom-call(bf16[8,256,128]{2,1,0:T(8,128)(2,1)} %x_ref.1, s32[8]{0:T(128)} %mask_ref.1, f32[1,128]{1,0:T(1,128)} %bitcast.11, bf16[128,512]{1,0:T(8,128)(2,1)} %w1_ref.1, f32[1,128]{1,0:T(1,128)} %bitcast.12, bf16[4,128]{1,0:T(4,128)(2,1)} %bitcast.9, bf16[128,128]{1,0:T(8,128)(2,1)} %ow1_ref.1, ...), custom_call_target="tpu_custom_call" | custom-call | tf_op jit(solution)/shard_map/pallas_call | solution.py:405
  58.5 1.9 %copy.18 = bf16[8,256,128]{2,1,0:T(8,128)(2,1)} copy(bf16[8,256,128]{2,1,0:T(8,128)(2,1)} %shard_map.154) | data formatting | bytes 1048576

commit v5 on v4

--- a/solution.py
+++ b/solution.py
@@ -351,6 +351,17 @@
                 turned + kb_ref[:, t * 128 : (t + 1) * 128]
             ) * LOG2E
 
+    te = min(tq, res // 2)
+
+    def spread_some(g, first, last):
+        part = pl.ds(pl.multiple_of(g * 2 * rows, 2 * rows), 2 * rows)
+
+        @pl.loop(first, last)
+        def _(p):
+            @pl.when(p != me)
+            def _():
+                share(4, send_z.at[p, part], recv_o.at[me, part], p).start()
+
     def end_pair(g, carry):
         ready = []
         for e in range(2):
@@ -361,28 +372,29 @@
             v = p[:, 2 * ch : 3 * ch].astype(BF16)
             gate = jax.nn.sigmoid(p[:, 3 * ch :] + gb2_ref[...])
             ready.append((z1, q, k, v, gate))
-        for s in range(res // tq):
-            lo = s * tq
+        for s in range(res // te):
+            lo = s * te
             blocks = []
             for z1, q, k, v, gate in ready:
-                o = attend(q[lo : lo + tq], k, v, bias_ref, lo, tq)
-                gated = (o * gate[lo : lo + tq]).astype(BF16)
-                z2 = z1[lo : lo + tq] + nn(gated, ow2_ref[...])
+                o = attend(q[lo : lo + te], k, v, bias_ref, lo, te)
+                gated = (o * gate[lo : lo + te]).astype(BF16)
+                z2 = z1[lo : lo + te] + nn(gated, ow2_ref[...])
                 z2 = z2.astype(BF16).astype(F32)
                 hid = nn(layer_norm(z2, g3_ref[...]), ti_ref[...]) + tb_ref[...]
                 hid = jnp.maximum(hid, 0.0).astype(BF16)
                 z3 = z2 + nn(hid, to_ref[...])
-                blocks.append(z3.reshape(tq // rows, rows, ch))
+                blocks.append(z3.reshape(te // rows, rows, ch))
             send_z[
-                lo // rows : (lo + tq) // rows,
+                lo // rows : (lo + te) // rows,
                 pl.ds(pl.multiple_of(g * 2 * rows, 2 * rows), 2 * rows),
                 :,
             ] = jnp.concatenate(blocks, axis=1).astype(BF16)
-        spread_pair(4, send_z, recv_o, g)
+            spread_some(g, lo // rows, (lo + te) // rows)
         return carry
 
     lax.fori_loop(0, rows // 2, end_pair, 0)
     spread_finish(4, send_z, recv_o)
+    recv_o[me] = send_z[me]
 
     zs_ref[...] = recv_o[...].astype(F32)
 

time: 60.6 us -> 64.3 us (1.061)
  Pallas kernels: 58.5 us -> 61.8 us
    pallas_call x1, Pallas kernels: 58.5 us -> 61.8 us  [local(): pl.pallas_call(functools.partial(kernel, nx, ny, tq), out_shape=jax.Shape...]
where the time goes in v5:
time: 64.3 us; the launch traced here: 63.7 us
  Pallas kernels  61.8 us (96%)
  local copies, waits for them, and re-layouts  1.87 us (3%)
    pallas_call x1, Pallas kernels, local(): pl.pallas_call(functools.partial(kernel, nx, ny, tq), out_shape=jax.Shape...  61.8 us
    unnamed x1, local copies, waits for them, and re-layouts  1.87 us

profile of v5, /device:TPU:0, one launch (start us, length us, event | category | flops | bytes accessed | tf_op | source)
XLA Modules:
  0.0 63.7 jit_solution(2730036119308241972)
XLA Ops:
  0.0 61.8 %shard_map.154 = bf16[8,256,128]{2,1,0:T(8,128)(2,1)} custom-call(bf16[8,256,128]{2,1,0:T(8,128)(2,1)} %x_ref.1, s32[8]{0:T(128)} %mask_ref.1, f32[1,128]{1,0:T(1,128)} %bitcast.11, bf16[128,512]{1,0:T(8,128)(2,1)} %w1_ref.1, f32[1,128]{1,0:T(1,128)} %bitcast.12, bf16[4,128]{1,0:T(4,128)(2,1)} %bitcast.9, bf16[128,128]{1,0:T(8,128)(2,1)} %ow1_ref.1, ...), custom_call_target="tpu_custom_call" | custom-call | tf_op jit(solution)/shard_map/pallas_call | solution.py:417
  61.8 1.9 %copy.18 = bf16[8,256,128]{2,1,0:T(8,128)(2,1)} copy(bf16[8,256,128]{2,1,0:T(8,128)(2,1)} %shard_map.154) | data formatting | bytes 1048576
